TPU v7x, 32 devices: a whole 2x2x4 slice. The times are simulated.
32 devices in a mesh: lat: 8 (over z, y), lon: 4 (over x, core).
Axes of the slice: x: 2, y: 2, z: 4, core: 2. Of those that a mesh axis runs over, the one named last changes fastest.
Arguments:
- features: bfloat16 [98304, 128], P(('lat', 'lon')), may hold values from -6 to 6
- cell_index: int32 [98304], P(('lat', 'lon')), may hold values from 0 to 2547
- tile_rows: int32 [1024], P(('lat', 'lon')), may hold values from 1 to 96, as said below
- spread: float32 [3, 3], replicated, may hold values from 0.2 to 1
- w_in: bfloat16 [128, 256], replicated, may hold values from -0.5 to 0.5
- w_dens: float32 [256], replicated, may hold values from -3 to 3
- w_one: bfloat16 [3, 3, 256, 256], replicated, may hold values from -0.125 to 0.125
- w_two: bfloat16 [3, 3, 256, 256], replicated, may hold values from -0.125 to 0.125
Outputs:
- encoded: bfloat16 [192, 384, 256], P('lat', 'lon')
Inputs may be any that keep to these rules, and one draw needn't show every extreme that they name: `tile_rows`: every block has 1 to 96 used slots; on every device some block has exactly 96.
All inputs are finite; a program needn't handle non-finite values.
Results may differ from a plain program's by a relative error of at most 0.0054.
Values may be sent and summed in bfloat16 or wider, within the bound.
A program may use at most 64 MiB of HBM per device.

v0:
```python
import jax
import jax.numpy as jnp
from jax import lax
from jax.sharding import PartitionSpec as P

TH = 24
TW = 96
F = 128
C = 256
CAP = 96
PH = 26
PW = 98


def padded_2(cells, sides, width):
    for axis, dim in sides:
        count = lax.axis_size(axis)
        head = lax.slice_in_dim(cells, 0, width, axis=dim)
        tail = lax.slice_in_dim(cells, cells.shape[dim] - width, cells.shape[dim], axis=dim)
        cells = jnp.concatenate(
            [
                lax.ppermute(tail, axis, [(i, (i + 1) % count) for i in range(count)]),
                cells,
                lax.ppermute(head, axis, [((i + 1) % count, i) for i in range(count)]),
            ],
            axis=dim,
        )
    return cells


def clear_edges(padded, width, tile_rows_count):
    lat_pos = lax.axis_index("lat")
    lat_count = lax.axis_size("lat")
    global_rows = jnp.arange(padded.shape[0], dtype=jnp.int32) + lat_pos * tile_rows_count - width
    keep = (global_rows >= 0) & (global_rows < lat_count * tile_rows_count)
    return jnp.where(keep[:, None, None], padded, jnp.zeros((), padded.dtype))


def conv_tile(padded, weight, out_rows, out_cols):
    chans = padded.shape[2]
    total = jnp.zeros((out_rows * out_cols, weight.shape[3]), jnp.float32)
    for row_off in range(3):
        for col_off in range(3):
            window = padded[row_off : row_off + out_rows, col_off : col_off + out_cols].reshape(
                -1, chans
            )
            total = total + jnp.dot(
                window, weight[row_off, col_off], preferred_element_type=jnp.float32
            )
    return total.reshape(out_rows, out_cols, -1)


def shards(features, cell_index, tile_rows, spread, w_in, w_dens, w_one, w_two):
    lat_count = lax.axis_size("lat")
    lon_count = lax.axis_size("lon")
    tiles = lat_count * lon_count
    frame_cells = PH * PW
    slot_ids = jnp.arange(CAP, dtype=jnp.int32)
    valid = slot_ids[None, :] < tile_rows[:, None]
    cells = jnp.where(valid, cell_index.reshape(tiles, CAP), frame_cells)
    got_rows, got_cells = (
        lax.all_to_all(
            features.reshape(tiles, CAP, F), ("lat", "lon"), split_axis=0, concat_axis=0, tiled=True
        ),
        lax.all_to_all(cells, ("lat", "lon"), split_axis=0, concat_axis=0, tiled=True),
    )
    received = tiles * CAP
    got_rows = got_rows.reshape(received, F)
    got_cells = got_cells.reshape(received)
    block_rows = 1024
    blocks = received // block_rows
    frame_ids = jnp.arange(frame_cells, dtype=jnp.int32)

    def add_block(carry, item):
        sums, counts = carry
        rows_blk, cells_blk = item
        onehot = frame_ids[:, None] == cells_blk[None, :]
        sums = sums + jnp.dot(
            onehot.astype(jnp.bfloat16), rows_blk, preferred_element_type=jnp.float32
        )
        counts = counts + jnp.sum(onehot.astype(jnp.float32), axis=1)
        return ((sums, counts), None)

    start_carry = (jnp.zeros((frame_cells, F), jnp.float32), jnp.zeros((frame_cells,), jnp.float32))
    (frame_sum, frame_count), _ = lax.scan(
        add_block,
        start_carry,
        (got_rows.reshape(blocks, block_rows, F), got_cells.reshape(blocks, block_rows)),
    )
    frame_sum = frame_sum.reshape(PH, PW, F)
    frame_count = frame_count.reshape(PH, PW)
    data = jnp.zeros((TH, TW, F), jnp.float32)
    density = jnp.zeros((TH, TW), jnp.float32)
    for row_off in range(3):
        for col_off in range(3):
            data = (
                data
                + spread[row_off, col_off]
                * frame_sum[row_off : row_off + TH, col_off : col_off + TW]
            )
            density = (
                density
                + spread[row_off, col_off]
                * frame_count[row_off : row_off + TH, col_off : col_off + TW]
            )
    mean = (data / (1.0 + density)[..., None]).astype(jnp.bfloat16)
    grid = jnp.dot(mean.reshape(-1, F), w_in, preferred_element_type=jnp.float32)
    grid = grid + jnp.log1p(density).reshape(-1, 1) * w_dens[None, :]
    grid = grid.astype(jnp.bfloat16).reshape(TH, TW, C)
    padded = clear_edges(padded_2(grid, (("lat", 0), ("lon", 1)), 1), 1, TH)
    hidden = jax.nn.silu(conv_tile(padded, w_one, TH, TW)).astype(jnp.bfloat16)
    hidden_pad = clear_edges(padded_2(hidden, (("lat", 0), ("lon", 1)), 1), 1, TH)
    encoded = grid.astype(jnp.float32) + conv_tile(hidden_pad, w_two, TH, TW)
    return encoded.astype(jnp.bfloat16)


def solution(mesh):
    in_specs = (
        P(("lat", "lon"), None),
        P(("lat", "lon")),
        P(("lat", "lon")),
        P(),
        P(),
        P(),
        P(),
        P(),
    )
    out_specs = P("lat", "lon", None)
    return jax.shard_map(shards, mesh=mesh, in_specs=in_specs, out_specs=out_specs, check_vma=False)
```

profile of v0, /device:TPU:0, one launch (start us, length us, event | category | flops | bytes accessed | tf_op | source)
XLA Modules:
  0.0 100.9 jit_solution(10324990009704199396)
XLA Ops:
  0.0 0.8 reshape.133
  0.8 0.8 compare_select_fusion
  1.6 14.3 %all_to_all.11 = s32[32,1,96]{2,1,0:T(1,128)S(1)} all-to-all(s32[32,1,96]{2,1,0:T(1,128)S(1)} %compare_select_fusion), channel_id=1, replica_groups=mesh['lat'=8,'lon'=4] {'lat','lon'}, dimensions={0} | all-to-all | bytes 24576 | tf_op jit(solution)/shard_map/all_to_all | solution.py:65
  15.9 2.6 %all-to-all-start.1 = ((bf16[32,96,128]{2,1,0:T(8,128)(2,1)}), bf16[32,96,128]{2,1,0:T(8,128)(2,1)S(1)}, u32[]{:S(2)}, u32[]{:S(2)}) async-start(bf16[32,96,128]{2,1,0:T(8,128)(2,1)} %bitcast.142), calls=%async_computation.1 | async-start | bytes 1572864 | tf_op jit(solution)/shard_map/all_to_all | solution.py:62
  18.6 0.7 fusion.72
  19.3 0.6 broadcast.76
  19.9 0.7 reduce.3
  20.6 0.1 reshape_reshape.6
  20.7 18.4 %all-to-all-done.1 = bf16[32,96,128]{2,1,0:T(8,128)(2,1)S(1)} async-done(((bf16[32,96,128]{2,1,0:T(8,128)(2,1)}), bf16[32,96,128]{2,1,0:T(8,128)(2,1)S(1)}, u32[]{:S(2)}, u32[]{:S(2)}) %all-to-all-start.1) | async-done | bytes 786464 | tf_op jit(solution)/shard_map/all_to_all | solution.py:62
  39.1 10.2 %while.13 = (s32[]{:T(128)}, f32[2548,128]{1,0:T(8,128)S(1)}, f32[2548]{0:T(1024)S(1)}, s32[3,1024]{1,0:T(4,128)S(1)}, bf16[3,1024,128]{2,1,0:T(8,128)(2,1)S(1)}, /*index=5*/s32[]{:T(128)}, s32[]{:T(128)}) while((s32[]{:T(128)}, f32[2548,128]{1,0:T(8,128)S(1)}, f32[2548]{0:T(1024)S(1)}, s32[3,1024]{1,0:T(4,128)S(1)}, ...), condition=%wide.region_2.3_spmd.clone, body=%wide.region_0.2_spmd.clone.sunk | while | flops 679034368 | bytes 2930600 | solution.py:85
  39.1 1.1 %fusion.98 = f32[2548]{0:T(1024)S(1)} fusion(s32[1024]{0:T(1024)S(1)} %bitcast.145), kind=kLoop, calls=%fused_computation.4.clone.1 | loop fusion | flops 7824908 | bytes 14288 | tf_op jit(solution)/shard_map/while/body/eval_jaxpr/reduce_sum | solution.py:81
  40.3 2.2 %fusion.97 = f32[2548,128]{1,0:T(8,128)S(1)} fusion(s32[1024]{0:T(1024)S(1)} %bitcast.146, f32[2548,128]{1,0:T(8,128)S(1)} %get-tuple-element.146, pred[]{:T(512)S(6)} %compare.3, bf16[3,1024,128]{2,1,0:T(8,128)(2,1)S(1)} %get-tuple-element.156, s32[]{:T(128)S(6)} %copy.12), kind=kOutput, calls=%fused_computation.6.clone.1 | convolution fusion | flops 671204352 | bytes 2877445 | tf_op jit(solution)/shard_map/while/body/eval_jaxpr/dot_general | solution.py:78
  42.5 1.1 %fusion.98 = f32[2548]{0:T(1024)S(1)} fusion(s32[1024]{0:T(1024)S(1)} %bitcast.145), kind=kLoop, calls=%fused_computation.4.clone.1 | loop fusion | flops 7824908 | bytes 14288 | tf_op jit(solution)/shard_map/while/body/eval_jaxpr/reduce_sum | solution.py:81
  43.7 2.2 %fusion.97 = f32[2548,128]{1,0:T(8,128)S(1)} fusion(s32[1024]{0:T(1024)S(1)} %bitcast.146, f32[2548,128]{1,0:T(8,128)S(1)} %get-tuple-element.146, pred[]{:T(512)S(6)} %compare.3, bf16[3,1024,128]{2,1,0:T(8,128)(2,1)S(1)} %get-tuple-element.156, s32[]{:T(128)S(6)} %copy.12), kind=kOutput, calls=%fused_computation.6.clone.1 | convolution fusion | flops 671204352 | bytes 2877445 | tf_op jit(solution)/shard_map/while/body/eval_jaxpr/dot_general | solution.py:78
  45.9 1.1 %fusion.98 = f32[2548]{0:T(1024)S(1)} fusion(s32[1024]{0:T(1024)S(1)} %bitcast.145), kind=kLoop, calls=%fused_computation.4.clone.1 | loop fusion | flops 7824908 | bytes 14288 | tf_op jit(solution)/shard_map/while/body/eval_jaxpr/reduce_sum | solution.py:81
  47.1 2.2 %fusion.97 = f32[2548,128]{1,0:T(8,128)S(1)} fusion(s32[1024]{0:T(1024)S(1)} %bitcast.146, f32[2548,128]{1,0:T(8,128)S(1)} %get-tuple-element.146, pred[]{:T(512)S(6)} %compare.3, bf16[3,1024,128]{2,1,0:T(8,128)(2,1)S(1)} %get-tuple-element.156, s32[]{:T(128)S(6)} %copy.12), kind=kOutput, calls=%fused_computation.6.clone.1 | convolution fusion | flops 671204352 | bytes 2877445 | tf_op jit(solution)/shard_map/while/body/eval_jaxpr/dot_general | solution.py:78
  49.3 0.1 reshape.136
  49.4 5.8 %fusion.67 = (f32[24,96]{1,0:T(8,128)S(1)}, f32[24,96]{1,0:T(8,128)S(1)}) fusion(f32[26,98]{1,0:T(8,128)S(1)} %reshape.136, f32[]{:T(128)} %bitcast.10, f32[]{:T(128)} %bitcast.9, f32[]{:T(128)} %bitcast.8, f32[]{:T(128)} %bitcast.7, f32[]{:T(128)} %bitcast.6, f32[]{:T(128)} %bitcast.5, f32[]{:T(128)} %bitcast.4, f32[]{:T(128)} %bitcast.3, f32[]{:T(128)} %bitcast), kind=kLoop, calls=%fused_computation.119 | loop fusion | flops 39168 | bytes 101412 | tf_op jit(solution)/shard_map/log1p | solution.py:108
  55.2 0.1 mul.167
  55.3 0.1 reshape.135
  55.3 0.0 copy-start.5
  55.4 7.0 %fusion.20 = bf16[24,96,128]{2,1,0:T(8,128)(2,1)S(1)} fusion(f32[26,98,128]{2,1,0:T(8,128)S(1)} %reshape.135, f32[24,96]{1,0:T(8,128)S(1)} %broadcast_add_fusion, f32[]{:T(128)} %bitcast.10, f32[]{:T(128)} %bitcast.9, f32[]{:T(128)} %bitcast.8, f32[]{:T(128)} %bitcast.7, f32[]{:T(128)} %bitcast.6, f32[]{:T(128)} %bitcast.5, f32[]{:T(128)} %bitcast.4, ...), kind=kLoop, calls=%fused_computation.52 | loop fusion | flops 5603328 | bytes 11215908 | tf_op jit(solution)/shard_map/convert_element_type | solution.py:106
  62.4 0.5 fusion.10
  62.9 1.6 %collective-permute-start = (bf16[1,96,256]{2,1,0:T(8,128)(2,1)S(1)}, bf16[1,96,256]{2,1,0:T(8,128)(2,1)S(1)}, u32[]{:S(2)}, u32[]{:S(2)}) collective-permute-start(bf16[1,96,256]{2,1,0:T(8,128)(2,1)S(1)} %get-tuple-element.96), channel_id=1, source_target_pairs={{0,4},{4,8},{8,12},{12,16},{16,20},{20,24},{24,28},{28,0},{1,5},{5... | collective-permute-start | bytes 147464 | tf_op jit(solution)/shard_map/ppermute | solution.py:22
  64.5 3.2 %collective-permute-start.1 = (bf16[1,96,256]{2,1,0:T(8,128)(2,1)S(1)}, bf16[1,96,256]{2,1,0:T(8,128)(2,1)S(1)}, u32[]{:S(2)}, u32[]{:S(2)}) collective-permute-start(bf16[1,96,256]{2,1,0:T(8,128)(2,1)S(1)} %get-tuple-element.97), channel_id=1, source_target_pairs={{4,0},{8,4},{12,8},{16,12},{20,16},{24,20},{28,24},{0,28},{5,1},{9... | collective-permute-start | bytes 147464 | tf_op jit(solution)/shard_map/ppermute | solution.py:24
  67.7 2.1 %collective-permute-done = bf16[1,96,256]{2,1,0:T(8,128)(2,1)S(1)} collective-permute-done((bf16[1,96,256]{2,1,0:T(8,128)(2,1)S(1)}, bf16[1,96,256]{2,1,0:T(8,128)(2,1)S(1)}, u32[]{:S(2)}, u32[]{:S(2)}) %collective-permute-start) | collective-permute-done | bytes 49184 | tf_op jit(solution)/shard_map/ppermute | solution.py:22
  69.8 0.1 collective-permute-start.2
  69.9 1.7 %collective-permute-start.3 = (bf16[26,1,256]{2,1,0:T(2,128)(2,1)S(1)}, bf16[26,1,256]{2,1,0:T(2,128)(2,1)S(1)}, u32[]{:S(2)}, u32[]{:S(2)}) collective-permute-start(bf16[26,1,256]{2,1,0:T(2,128)(2,1)S(1)} %get-tuple-element.93), channel_id=1, source_target_pairs={{1,0},{2,1},{3,2},{0,3},{5,4},{6,5},{7,6},{4,7},{9,8},{10,9},{11,1... | collective-permute-start | bytes 39944 | tf_op jit(solution)/shard_map/ppermute | solution.py:24
  71.6 1.5 %collective-permute-done.2 = bf16[26,1,256]{2,1,0:T(2,128)(2,1)S(1)} collective-permute-done((bf16[26,1,256]{2,1,0:T(2,128)(2,1)S(1)}, bf16[26,1,256]{2,1,0:T(2,128)(2,1)S(1)}, u32[]{:S(2)}, u32[]{:S(2)}) %collective-permute-start.2) | collective-permute-done | bytes 13344 | tf_op jit(solution)/shard_map/ppermute | solution.py:22
  73.1 0.0 collective-permute-done.3
  73.1 0.8 maximum_select_fusion
  73.9 0.0 copy-start.2
  74.0 2.5 %fusion.70 = (bf16[24,96,256]{2,1,0:T(8,128)(2,1)S(1)}, bf16[24,96,256]{2,1,0:T(8,128)(2,1)S(1)}, bf16[24,96,256]{2,1,0:T(8,128)(2,1)S(1)}, bf16[24,96,256]{2,1,...) fusion(bf16[26,98,256]{2,1,0:T(8,128)(2,1)S(1)} %maximum_select, ...), kind=kLoop, calls=%fused_computation.121 | loop fusion | bytes 21233664 | tf_op jit(solution)/shard_map/slice | solution.py:44
  76.5 0.5 fusion.39
  76.9 0.5 convolution_add_fusion.15
  77.4 0.5 convolution_add_fusion.14
  77.9 0.5 convolution_add_fusion.13
  78.4 0.5 convolution_add_fusion.12
  78.8 0.5 convolution_add_fusion.11
  79.3 0.5 convolution_add_fusion.10
  79.8 0.5 convolution_add_fusion.9
  80.3 0.5 convolution_add_fusion.8
  80.7 0.7 multiply_convert_fusion
  81.4 1.2 %collective-permute-start.4 = (bf16[1,96,256]{2,1,0:T(8,128)(2,1)S(1)}, bf16[1,96,256]{2,1,0:T(8,128)(2,1)S(1)}, u32[]{:S(2)}, u32[]{:S(2)}) collective-permute-start(bf16[1,96,256]{2,1,0:T(8,128)(2,1)S(1)} %get-tuple-element.94), channel_id=1, source_target_pairs={{0,4},{4,8},{8,12},{12,16},{16,20},{20,24},{24,28},{28,0},{1,5},{5... | collective-permute-start | bytes 147464 | tf_op jit(solution)/shard_map/ppermute | solution.py:22
  82.6 3.7 %collective-permute-start.5 = (bf16[1,96,256]{2,1,0:T(8,128)(2,1)S(1)}, bf16[1,96,256]{2,1,0:T(8,128)(2,1)S(1)}, u32[]{:S(2)}, u32[]{:S(2)}) collective-permute-start(bf16[1,96,256]{2,1,0:T(8,128)(2,1)S(1)} %get-tuple-element.95), channel_id=1, source_target_pairs={{4,0},{8,4},{12,8},{16,12},{20,16},{24,20},{28,24},{0,28},{5,1},{9... | collective-permute-start | bytes 147464 | tf_op jit(solution)/shard_map/ppermute | solution.py:24
  86.3 2.0 %collective-permute-done.4 = bf16[1,96,256]{2,1,0:T(8,128)(2,1)S(1)} collective-permute-done((bf16[1,96,256]{2,1,0:T(8,128)(2,1)S(1)}, bf16[1,96,256]{2,1,0:T(8,128)(2,1)S(1)}, u32[]{:S(2)}, u32[]{:S(2)}) %collective-permute-start.4) | collective-permute-done | bytes 49184 | tf_op jit(solution)/shard_map/ppermute | solution.py:22
  88.3 0.8 collective-permute-start.6
  89.1 1.2 %collective-permute-start.7 = (bf16[26,1,256]{2,1,0:T(2,128)(2,1)S(1)}, bf16[26,1,256]{2,1,0:T(2,128)(2,1)S(1)}, u32[]{:S(2)}, u32[]{:S(2)}) collective-permute-start(bf16[26,1,256]{2,1,0:T(2,128)(2,1)S(1)} %get-tuple-element.91), channel_id=1, source_target_pairs={{1,0},{2,1},{3,2},{0,3},{5,4},{6,5},{7,6},{4,7},{9,8},{10,9},{11,1... | collective-permute-start | bytes 39944 | tf_op jit(solution)/shard_map/ppermute | solution.py:24
  90.3 1.3 %collective-permute-done.6 = bf16[26,1,256]{2,1,0:T(2,128)(2,1)S(1)} collective-permute-done((bf16[26,1,256]{2,1,0:T(2,128)(2,1)S(1)}, bf16[26,1,256]{2,1,0:T(2,128)(2,1)S(1)}, u32[]{:S(2)}, u32[]{:S(2)}) %collective-permute-start.6) | collective-permute-done | bytes 13344 | tf_op jit(solution)/shard_map/ppermute | solution.py:22
  91.7 0.2 collective-permute-done.7
  91.9 0.8 maximum_select_fusion.1
  92.7 0.0 copy-start.3
  92.7 2.5 %fusion.69 = (bf16[24,96,256]{2,1,0:T(8,128)(2,1)S(1)}, bf16[24,96,256]{2,1,0:T(8,128)(2,1)S(1)}, bf16[24,96,256]{2,1,0:T(8,128)(2,1)S(1)}, bf16[24,96,256]{2,1,...) fusion(bf16[26,98,256]{2,1,0:T(8,128)(2,1)S(1)} %maximum_select, ...), kind=kLoop, calls=%fused_computation.120 | loop fusion | bytes 21233664 | tf_op jit(solution)/shard_map/slice | solution.py:44
  95.2 0.5 fusion.29
  95.6 0.5 convolution_add_fusion.7
  96.1 0.5 convolution_add_fusion.6
  96.6 0.5 convolution_add_fusion.5
  97.1 0.5 convolution_add_fusion.4
  97.6 0.5 convolution_add_fusion.3
  98.0 0.5 convolution_add_fusion.2
  98.5 0.5 convolution_add_fusion.1
  99.0 0.5 convolution_add_fusion
  99.5 0.0 copy-start.1
  99.5 1.4 %add_convert_fusion = bf16[24,96,256]{2,1,0:T(8,128)(2,1)} fusion(f32[24,96,256]{2,1,0:T(8,128)S(1)} %bitcast.122, bf16[24,96,256]{2,1,0:T(8,128)(2,1)S(1)} %bitcast.121), kind=kLoop, calls=%fused_computation.30 | loop fusion | flops 1769472 | bytes 4718592 | tf_op jit(solution)/shard_map/convert_element_type | solution.py:114
  (24 shorter events, 0.2 us)
Async XLA Ops:
  0.0 62.4 %copy-start = (bf16[128,256]{1,0:T(8,128)(2,1)S(1)}, bf16[128,256]{1,0:T(8,128)(2,1)}, u32[]{:S(2)}) copy-start(bf16[128,256]{1,0:T(8,128)(2,1)} %param.14) | copy-start | bytes 196612
  0.0 18.6 %copy-start.4 = (f32[3,3]{1,0:T(4,128)S(1)}, f32[3,3]{1,0:T(4,128)}, u32[]{:S(2)}) copy-start(f32[3,3]{1,0:T(4,128)} %param.13) | copy-start | bytes 112
  15.9 23.2 %all-to-all-start.1 = ((bf16[32,96,128]{2,1,0:T(8,128)(2,1)}), bf16[32,96,128]{2,1,0:T(8,128)(2,1)S(1)}, u32[]{:S(2)}, u32[]{:S(2)}) async-start(bf16[32,96,128]{2,1,0:T(8,128)(2,1)} %bitcast.142), calls=%async_computation.1 | async-start | bytes 1572864 | tf_op jit(solution)/shard_map/all_to_all | solution.py:62
  55.3 7.1 %copy-start.5 = (f32[256]{0:T(256)S(1)}, f32[256]{0:T(256)}, u32[]{:S(2)}) copy-start(f32[256]{0:T(256)} %param.15) | copy-start | bytes 3076
  62.9 6.8 %collective-permute-start = (bf16[1,96,256]{2,1,0:T(8,128)(2,1)S(1)}, bf16[1,96,256]{2,1,0:T(8,128)(2,1)S(1)}, u32[]{:S(2)}, u32[]{:S(2)}) collective-permute-start(bf16[1,96,256]{2,1,0:T(8,128)(2,1)S(1)} %get-tuple-element.96), channel_id=1, source_target_pairs={{0,4},{4,8},{8,12},{12,16},{16,20},{20,24},{24,28},{28,0},{1,5},{5... | collective-permute-start | bytes 147464 | tf_op jit(solution)/shard_map/ppermute | solution.py:22
  64.5 5.2 %collective-permute-start.1 = (bf16[1,96,256]{2,1,0:T(8,128)(2,1)S(1)}, bf16[1,96,256]{2,1,0:T(8,128)(2,1)S(1)}, u32[]{:S(2)}, u32[]{:S(2)}) collective-permute-start(bf16[1,96,256]{2,1,0:T(8,128)(2,1)S(1)} %get-tuple-element.97), channel_id=1, source_target_pairs={{4,0},{8,4},{12,8},{16,12},{20,16},{24,20},{28,24},{0,28},{5,1},{9... | collective-permute-start | bytes 147464 | tf_op jit(solution)/shard_map/ppermute | solution.py:24
  69.8 3.3 %collective-permute-start.2 = (bf16[26,1,256]{2,1,0:T(2,128)(2,1)S(1)}, bf16[26,1,256]{2,1,0:T(2,128)(2,1)S(1)}, u32[]{:S(2)}, u32[]{:S(2)}) collective-permute-start(bf16[26,1,256]{2,1,0:T(2,128)(2,1)S(1)} %get-tuple-element.92), channel_id=1, source_target_pairs={{0,1},{1,2},{2,3},{3,0},{4,5},{5,6},{6,7},{7,4},{8,9},{9,10},{10,1... | collective-permute-start | bytes 39944 | tf_op jit(solution)/shard_map/ppermute | solution.py:22
  69.9 3.3 %collective-permute-start.3 = (bf16[26,1,256]{2,1,0:T(2,128)(2,1)S(1)}, bf16[26,1,256]{2,1,0:T(2,128)(2,1)S(1)}, u32[]{:S(2)}, u32[]{:S(2)}) collective-permute-start(bf16[26,1,256]{2,1,0:T(2,128)(2,1)S(1)} %get-tuple-element.93), channel_id=1, source_target_pairs={{1,0},{2,1},{3,2},{0,3},{5,4},{6,5},{7,6},{4,7},{9,8},{10,9},{11,1... | collective-permute-start | bytes 39944 | tf_op jit(solution)/shard_map/ppermute | solution.py:24
  73.9 2.5 %copy-start.2 = (bf16[3,3,256,256]{3,2,1,0:T(8,128)(2,1)S(1)}, bf16[3,3,256,256]{3,2,1,0:T(8,128)(2,1)}, u32[]{:S(2)}) copy-start(bf16[3,3,256,256]{3,2,1,0:T(8,128)(2,1)} %param.16) | copy-start | bytes 3538948
  81.4 6.9 %collective-permute-start.4 = (bf16[1,96,256]{2,1,0:T(8,128)(2,1)S(1)}, bf16[1,96,256]{2,1,0:T(8,128)(2,1)S(1)}, u32[]{:S(2)}, u32[]{:S(2)}) collective-permute-start(bf16[1,96,256]{2,1,0:T(8,128)(2,1)S(1)} %get-tuple-element.94), channel_id=1, source_target_pairs={{0,4},{4,8},{8,12},{12,16},{16,20},{20,24},{24,28},{28,0},{1,5},{5... | collective-permute-start | bytes 147464 | tf_op jit(solution)/shard_map/ppermute | solution.py:22
  82.6 5.7 %collective-permute-start.5 = (bf16[1,96,256]{2,1,0:T(8,128)(2,1)S(1)}, bf16[1,96,256]{2,1,0:T(8,128)(2,1)S(1)}, u32[]{:S(2)}, u32[]{:S(2)}) collective-permute-start(bf16[1,96,256]{2,1,0:T(8,128)(2,1)S(1)} %get-tuple-element.95), channel_id=1, source_target_pairs={{4,0},{8,4},{12,8},{16,12},{20,16},{24,20},{28,24},{0,28},{5,1},{9... | collective-permute-start | bytes 147464 | tf_op jit(solution)/shard_map/ppermute | solution.py:24
  88.3 3.3 %collective-permute-start.6 = (bf16[26,1,256]{2,1,0:T(2,128)(2,1)S(1)}, bf16[26,1,256]{2,1,0:T(2,128)(2,1)S(1)}, u32[]{:S(2)}, u32[]{:S(2)}) collective-permute-start(bf16[26,1,256]{2,1,0:T(2,128)(2,1)S(1)} %get-tuple-element.90), channel_id=1, source_target_pairs={{0,1},{1,2},{2,3},{3,0},{4,5},{5,6},{6,7},{7,4},{8,9},{9,10},{10,1... | collective-permute-start | bytes 39944 | tf_op jit(solution)/shard_map/ppermute | solution.py:22
  89.1 2.8 %collective-permute-start.7 = (bf16[26,1,256]{2,1,0:T(2,128)(2,1)S(1)}, bf16[26,1,256]{2,1,0:T(2,128)(2,1)S(1)}, u32[]{:S(2)}, u32[]{:S(2)}) collective-permute-start(bf16[26,1,256]{2,1,0:T(2,128)(2,1)S(1)} %get-tuple-element.91), channel_id=1, source_target_pairs={{1,0},{2,1},{3,2},{0,3},{5,4},{6,5},{7,6},{4,7},{9,8},{10,9},{11,1... | collective-permute-start | bytes 39944 | tf_op jit(solution)/shard_map/ppermute | solution.py:24
  92.7 2.5 %copy-start.3 = (bf16[3,3,256,256]{3,2,1,0:T(8,128)(2,1)S(1)}, bf16[3,3,256,256]{3,2,1,0:T(8,128)(2,1)}, u32[]{:S(2)}) copy-start(bf16[3,3,256,256]{3,2,1,0:T(8,128)(2,1)} %param.17) | copy-start | bytes 3538948
  99.5 1.5 %copy-start.1 = (bf16[128,256]{1,0:T(8,128)(2,1)S(1)}, bf16[128,256]{1,0:T(8,128)(2,1)}, u32[]{:S(2)}) copy-start(bf16[128,256]{1,0:T(8,128)(2,1)} %param.14) | copy-start | bytes 196612
where the time goes:
time: 103 us; the launch traced here: 101 us
  waiting for transfers between devices  25.6 us (25%)
  other arithmetic  21.5 us (21%)
  starting transfers between devices  16 us (16%)
  matrix products  15.6 us (15%)
  blocking collectives  14.3 us (14%)
  local copies, waits for them, and re-layouts  7.5 us (7%)
    all_to_all x1, waiting for transfers between devices, shards(): lax.all_to_all(features.reshape(tiles, CAP, F), ('lat', 'lon'), split_axi...  18.4 us
    all_to_all x1, blocking collectives, shards(): lax.all_to_all(cells, ('lat', 'lon'), split_axis=0, concat_axis=0, tiled=...  14.3 us
    ppermute x4, starting transfers between devices, padded_2(): lax.ppermute(head, axis, [((i + 1) % count, i) for i in range(count)])  9.79 us
    dot_general x18, matrix products, conv_tile(): jnp.dot(window, weight[row_off, col_off], preferred_element_type=jnp.floa...  8.48 us
    convert_element_type x1, other arithmetic, shards(): mean = (data / (1.0 + density)[..., None]).astype(jnp.bfloat16)  7.02 us
    ppermute x4, waiting for transfers between devices, padded_2(): lax.ppermute(tail, axis, [(i, (i + 1) % count) for i in range(count)])  6.92 us
    dot_general x3, matrix products, add_block(): jnp.dot(onehot.astype(jnp.bfloat16), rows_blk, preferred_element_type=jnp...  6.61 us
    log1p x1, other arithmetic, shards(): grid = grid + jnp.log1p(density).reshape(-1, 1) * w_dens[None, :]  5.76 us
  transfers between devices with their start and end apart: 9, of which 6 were waited for; matrix products, arithmetic and copies ran while one was open for 2% of the time, Pallas kernels for 0%

commit v1 on v0

v1 whole, which is shorter than its diff:
```python
import functools

import jax
import jax.numpy as jnp
from jax import lax
from jax.experimental import pallas as pl
from jax.experimental.pallas import tpu as pltpu
from jax.sharding import PartitionSpec as P

TH = 24
TW = 96
F = 128
C = 256
CAP = 96
PH = 26
PW = 98
PWP = 112
GROUP = 8
HALF = PH // 2
ROWS = 8
MESH = pl.DeviceIdType.MESH
F32 = jnp.float32
BF16 = jnp.bfloat16


def xor(a, b, count):
    out = 0
    bit = 1
    while bit < count:
        out = out + ((a // bit + b // bit) % 2) * bit
        bit *= 2
    return out


def kernel(
    lat_n, lon_n,
    feats, cells, spread, w_in, w_dens, w_one, w_two, out,
    rows_in, cells_in, lhs, acc, mean, logd, grid_x, hid_x, win_v, wone_v, wtwo_v,
    row_out, row_in, col_out, col_in, corner_in,
    row_send, row_recv, cell_send, cell_recv, own_sem, w_sem, halo_send, halo_recv,
):
    n = lat_n * lon_n
    groups = n // GROUP
    lat = lax.axis_index("lat")
    lon = lax.axis_index("lon")
    me = lat * lon_n + lon
    my_group = me // GROUP
    my_place = me % GROUP
    east = (lon + 1) % lon_n
    west = (lon + lon_n - 1) % lon_n

    barrier = pltpu.get_barrier_semaphore()

    @pl.loop(1, n)
    def _(k):
        peer = (me + k) % n
        pl.semaphore_signal(
            barrier, inc=1, device_id=(peer // lon_n, peer % lon_n), device_id_type=MESH
        )

    own = [
        pltpu.make_async_copy(feats.at[me], rows_in.at[me], own_sem.at[0]),
        pltpu.make_async_copy(cells.at[me], cells_in.at[me], own_sem.at[1]),
    ]
    weights = [
        pltpu.make_async_copy(w_in, win_v, w_sem.at[0]),
        pltpu.make_async_copy(w_one, wone_v, w_sem.at[1]),
        pltpu.make_async_copy(w_two, wtwo_v, w_sem.at[2]),
    ]
    for item in own + weights:
        item.start()
    pl.semaphore_wait(barrier, n - 1)

    def row_copy(src_block, slot, peer):
        return pltpu.make_async_remote_copy(
            src_ref=feats.at[src_block], dst_ref=rows_in.at[slot],
            send_sem=row_send.at[src_block], recv_sem=row_recv.at[slot],
            device_id=(peer // lon_n, peer % lon_n), device_id_type=MESH,
        )

    def cell_copy(src_block, slot, peer):
        return pltpu.make_async_remote_copy(
            src_ref=cells.at[src_block], dst_ref=cells_in.at[slot],
            send_sem=cell_send.at[src_block], recv_sem=cell_recv.at[slot],
            device_id=(peer // lon_n, peer % lon_n), device_id_type=MESH,
        )

    def peer_of(step):
        turn = groups - 1 - step // GROUP
        return xor(my_group, turn, groups) * GROUP + (my_place + step % GROUP) % GROUP

    def each_peer(act):
        @pl.loop(0, n - GROUP)
        def _(step):
            act(peer_of(step))

        for place in range(1, GROUP):
            act(my_group * GROUP + (my_place + place) % GROUP)

    def send(peer):
        cell_copy(peer, me, peer).start()
        row_copy(peer, me, peer).start()

    each_peer(send)

    acc[...] = jnp.zeros_like(acc)

    def add_group(base):
        enc = jnp.concatenate([cells_in[base + m][:, :CAP] for m in range(GROUP)], axis=1)
        wide = GROUP * CAP
        col = jnp.broadcast_to(enc & 127, (PWP, wide))
        col_hot = jnp.where(
            lax.broadcasted_iota(jnp.int32, (PWP, wide), 0) == col, 1.0, 0.0
        ).astype(BF16)
        row = jnp.broadcast_to(enc >> 7, (16, wide))
        rows = rows_in[pl.ds(base, GROUP)].reshape(wide, F)
        rhs = jnp.concatenate([rows, jnp.ones((wide, C - F), BF16)], axis=1)
        col_hot = col_hot.reshape(PWP // 16, 16, wide)
        for r in range(PH):
            here = jnp.where(row == r, 1.0, 0.0).astype(BF16)
            lhs[r] = (col_hot * here[None]).reshape(PWP, wide)
        for half in range(2):
            span = slice(half * HALF, (half + 1) * HALF)
            part = jnp.dot(
                lhs[span].reshape(HALF * PWP, wide), rhs, preferred_element_type=F32
            )
            acc[span] += part.reshape(HALF, PWP, C)

    @pl.loop(0, groups - 1)
    def _(step):
        base = xor(my_group, groups - 1 - step, groups) * GROUP
        for m in range(GROUP):
            cell_copy(base + m, base + m, base + m).wait_recv()
            row_copy(base + m, base + m, base + m).wait_recv()
        add_group(base)

    for place in range(1, GROUP):
        peer = my_group * GROUP + (my_place + place) % GROUP
        cell_copy(peer, peer, peer).wait_recv()
        row_copy(peer, peer, peer).wait_recv()
    for item in own:
        item.wait()
    add_group(my_group * GROUP)

    weights[0].wait()

    def put(x_ref, stage, r, value):
        x_ref[r + 1, :, C : 2 * C] = value.astype(BF16)
        x_ref[r + 1, :, 0:C] = pltpu.roll(value, 1, 0).astype(BF16)
        x_ref[r + 1, :, 2 * C :] = pltpu.roll(value, TW - 1, 0).astype(BF16)
        col_out[stage, 0, pl.ds(r, 1)] = value[0:1]
        col_out[stage, 1, pl.ds(r, 1)] = value[TW - 1 : TW]

    @pl.loop(0, TH)
    def _(r):
        parts = []
        for b in range(3):
            parts.append(
                sum(spread[a, b] * acc[r + a, 0:104] for a in range(3))
            )
        total = parts[0][0:TW] + parts[1][1 : TW + 1] + parts[2][2 : TW + 2]
        level = 1.0 + total[:, F:]
        mean[r] = (total[:, :F] / level).astype(BF16)
        logd[r] = jnp.log(level)

    @pl.loop(0, TH // ROWS)
    def _(step):
        start = step * ROWS
        grid = jnp.dot(
            mean[pl.ds(start, ROWS)].reshape(ROWS * TW, F), win_v[...],
            preferred_element_type=F32,
        ).reshape(ROWS, TW, C)
        for k in range(ROWS):
            lg = logd[start + k]
            value = grid[k] + jnp.concatenate([lg, lg], axis=1) * w_dens[...]
            put(grid_x, 0, start + k, value)

    def halo_copy(stage, kind, src, dst, where):
        return pltpu.make_async_remote_copy(
            src_ref=src, dst_ref=dst,
            send_sem=halo_send.at[stage, kind], recv_sem=halo_recv.at[stage, kind],
            device_id=where, device_id_type=MESH,
        )

    def copies(stage, x_ref):
        up, down = lat - 1, lat + 1
        left, right = col_out.at[stage, 0], col_out.at[stage, 1]
        both = [
            halo_copy(stage, 0, right, col_in.at[stage, 0], (lat, east)),
            halo_copy(stage, 1, left, col_in.at[stage, 1], (lat, west)),
        ]
        low, high = pl.ds(0, 8), pl.ds(TH - 8, 8)
        to_up = [
            halo_copy(stage, 2, row_out.at[stage, 0], row_in.at[stage, 1], (up, lon)),
            halo_copy(stage, 3, right.at[low], corner_in.at[stage, 2], (up, east)),
            halo_copy(stage, 4, left.at[low], corner_in.at[stage, 3], (up, west)),
        ]
        to_down = [
            halo_copy(stage, 5, row_out.at[stage, 1], row_in.at[stage, 0], (down, lon)),
            halo_copy(stage, 6, right.at[high], corner_in.at[stage, 0], (down, east)),
            halo_copy(stage, 7, left.at[high], corner_in.at[stage, 1], (down, west)),
        ]
        return both, to_up, to_down

    def set_edges(x_ref, r, left, right):
        ids = lax.broadcasted_iota(jnp.int32, (16, C), 0)
        first = x_ref[r, 0:16, 0:C].astype(F32)
        x_ref[r, 0:16, 0:C] = jnp.where(ids == 0, left, first).astype(BF16)
        last = x_ref[r, TW - 16 : TW, 2 * C :].astype(F32)
        x_ref[r, TW - 16 : TW, 2 * C :] = jnp.where(ids == 15, right, last).astype(BF16)

    def exchange(stage, x_ref):
        row_out[stage, 0] = x_ref[1, :, C : 2 * C]
        row_out[stage, 1] = x_ref[TH, :, C : 2 * C]
        both, to_up, to_down = copies(stage, x_ref)
        for item in both:
            item.start()

        @pl.when(lat > 0)
        def _():
            for item in to_up:
                item.start()

        @pl.when(lat < lat_n - 1)
        def _():
            for item in to_down:
                item.start()

        for item in both:
            item.wait_recv()

        @pl.loop(0, TH)
        def _(r):
            set_edges(
                x_ref, r + 1, col_in[stage, 0, pl.ds(r, 1)], col_in[stage, 1, pl.ds(r, 1)]
            )

        def outer(r, side, corner_row):
            value = row_in[stage, side].astype(F32)
            x_ref[r, :, C : 2 * C] = row_in[stage, side]
            x_ref[r, :, 0:C] = pltpu.roll(value, 1, 0).astype(BF16)
            x_ref[r, :, 2 * C :] = pltpu.roll(value, TW - 1, 0).astype(BF16)
            rows = slice(corner_row, corner_row + 1)
            set_edges(
                x_ref, r, corner_in[stage, 2 * side, rows], corner_in[stage, 2 * side + 1, rows]
            )

        @pl.when(lat > 0)
        def _():
            for item in to_down:
                item.wait_recv()
            outer(0, 0, 7)

        @pl.when(lat == 0)
        def _():
            x_ref[0] = jnp.zeros((TW, 3 * C), BF16)

        @pl.when(lat < lat_n - 1)
        def _():
            for item in to_up:
                item.wait_recv()
            outer(TH + 1, 1, 0)

        @pl.when(lat == lat_n - 1)
        def _():
            x_ref[TH + 1] = jnp.zeros((TW, 3 * C), BF16)

        for item in both:
            item.wait_send()

        @pl.when(lat > 0)
        def _():
            for item in to_up:
                item.wait_send()

        @pl.when(lat < lat_n - 1)
        def _():
            for item in to_down:
                item.wait_send()

    def conv(x_ref, weight, start):
        window = jnp.concatenate(
            [x_ref[pl.ds(start + a, ROWS)].reshape(ROWS * TW, 3 * C) for a in range(3)], axis=1
        )
        return jnp.dot(window, weight[...], preferred_element_type=F32).reshape(ROWS, TW, C)

    exchange(0, grid_x)
    weights[1].wait()

    @pl.loop(0, TH // ROWS)
    def _(step):
        start = step * ROWS
        total = conv(grid_x, wone_v, start)
        for k in range(ROWS):
            value = total[k]
            put(hid_x, 1, start + k, value / (1.0 + jnp.exp(-value)))

    exchange(1, hid_x)
    weights[2].wait()

    @pl.loop(0, TH // ROWS)
    def _(step):
        start = step * ROWS
        total = conv(hid_x, wtwo_v, start)
        base = grid_x[pl.ds(start + 1, ROWS), :, C : 2 * C].astype(F32)
        out[pl.ds(start, ROWS)] = (base + total).astype(BF16)

    def sent(peer):
        cell_copy(peer, me, peer).wait_send()
        row_copy(peer, me, peer).wait_send()

    each_peer(sent)


def shards(features, cell_index, tile_rows, spread, w_in, w_dens, w_one, w_two):
    lat_n = lax.axis_size("lat")
    lon_n = lax.axis_size("lon")
    n = lat_n * lon_n
    cell = cell_index.reshape(n, CAP)
    used = jnp.arange(CAP, dtype=jnp.int32)[None, :] < tile_rows[:, None]
    code = jnp.where(used, (cell // PW) * 128 + cell % PW, 127 * 128)
    code = jnp.pad(code, ((0, 0), (0, 128 - CAP))).reshape(n, 1, 128)
    anywhere = pl.BlockSpec(memory_space=pl.ANY)
    vmem = pl.BlockSpec(memory_space=pltpu.VMEM)
    smem = pl.BlockSpec(memory_space=pltpu.SMEM)
    dma = pltpu.SemaphoreType.DMA
    return pl.pallas_call(
        functools.partial(kernel, lat_n, lon_n),
        out_shape=jax.ShapeDtypeStruct((TH, TW, C), BF16),
        in_specs=[anywhere, anywhere, smem, anywhere, vmem, anywhere, anywhere],
        out_specs=vmem,
        scratch_shapes=[
            pltpu.VMEM((n, CAP, F), BF16),
            pltpu.VMEM((n, 1, 128), jnp.int32),
            pltpu.VMEM((PH, PWP, GROUP * CAP), BF16),
            pltpu.VMEM((PH, PWP, C), F32),
            pltpu.VMEM((TH, TW, F), BF16),
            pltpu.VMEM((TH, TW, F), F32),
            pltpu.VMEM((TH + 2, TW, 3 * C), BF16),
            pltpu.VMEM((TH + 2, TW, 3 * C), BF16),
            pltpu.VMEM((F, C), BF16),
            pltpu.VMEM((9 * C, C), BF16),
            pltpu.VMEM((9 * C, C), BF16),
            pltpu.VMEM((2, 2, TW, C), BF16),
            pltpu.VMEM((2, 2, TW, C), BF16),
            pltpu.VMEM((2, 2, TH, C), F32),
            pltpu.VMEM((2, 2, TH, C), F32),
            pltpu.VMEM((2, 4, 8, C), F32),
            dma((n,)), dma((n,)), dma((n,)), dma((n,)),
            dma((2,)), dma((3,)), dma((2, 8)), dma((2, 8)),
        ],
        compiler_params=pltpu.CompilerParams(
            collective_id=0, has_side_effects=True, vmem_limit_bytes=60 * 1024 * 1024
        ),
    )(
        features.reshape(n, CAP, F), code, spread, w_in, w_dens.reshape(1, C),
        w_one.reshape(9 * C, C), w_two.reshape(9 * C, C),
    )


def solution(mesh):
    blocks = P(("lat", "lon"))
    in_specs = (P(("lat", "lon"), None), blocks, blocks, P(), P(), P(), P(), P())
    out_specs = P("lat", "lon", None)
    return jax.shard_map(shards, mesh=mesh, in_specs=in_specs, out_specs=out_specs, check_vma=False)
```

time: 103 us -> 57.3 us (0.56); the launches traced: 101 us -> 56.8 us
  Pallas kernels: 0 us -> 51.4 us
  waiting for transfers between devices: 25.6 us -> 0 us
  other arithmetic: 21.5 us -> 2.16 us
  starting transfers between devices: 16 us -> 0 us
  matrix products: 15.6 us -> 0 us
  blocking collectives: 14.3 us -> 0 us
  local copies, waits for them, and re-layouts: 7.5 us -> 3.2 us
    pallas_call x0 -> x1, Pallas kernels: none -> 51.4 us  [shards(): pl.pallas_call(functools.partial(kernel, lat_n, lon_n), out_shape=jax.Sha...]
    all_to_all x1 -> x0, waiting for transfers between devices: 18.4 us -> none  [shards(): lax.all_to_all(features.reshape(tiles, CAP, F), ('lat', 'lon'), split_axi...]
    dot_general x22 -> x0, matrix products: 15.6 us -> none  [the longest x18 8.48 us: conv_tile(): jnp.dot(window, weight[row_off, col_off], preferred_element_type=jnp.floa...]
    all_to_all x1 -> x0, blocking collectives: 14.3 us -> none  [shards(): lax.all_to_all(cells, ('lat', 'lon'), split_axis=0, concat_axis=0, tiled=...]
    ppermute x8 -> x0, starting transfers between devices: 13.4 us -> none  [the longest x4 9.79 us: padded_2(): lax.ppermute(head, axis, [((i + 1) % count, i) for i in range(count)])]
    convert_element_type x3 -> x0, other arithmetic: 9.13 us -> none  [the longest x1 7.02 us: shards(): mean = (data / (1.0 + density)[..., None]).astype(jnp.bfloat16)]
    ppermute x8 -> x0, waiting for transfers between devices: 7.14 us -> none  [the longest x4 6.92 us: padded_2(): lax.ppermute(tail, axis, [(i, (i + 1) % count) for i in range(count)])]
    log1p x1 -> x0, other arithmetic: 5.76 us -> none  [shards(): grid = grid + jnp.log1p(density).reshape(-1, 1) * w_dens[None, :]]
  transfers between devices with their start and end apart: 9 -> 0, of which waited for: 6 -> 0; matrix products, arithmetic and copies ran while one was open for 2% -> 0% of each run, Pallas kernels for 0% -> 0%
where the time goes in v1:
time: 57.3 us; the launch traced here: 56.8 us
  Pallas kernels  51.4 us (90%)
  local copies, waits for them, and re-layouts  3.2 us (6%)
  other arithmetic  2.16 us (4%)
    pallas_call x1, Pallas kernels, shards(): pl.pallas_call(functools.partial(kernel, lat_n, lon_n), out_shape=jax.Sha...  51.4 us
    unnamed x1, local copies, waits for them, and re-layouts  2.36 us

profile of v1, /device:TPU:0, one launch (start us, length us, event | category | flops | bytes accessed | tf_op | source)
XLA Modules:
  0.0 56.8 jit_solution(6781494899844831980)
XLA Ops:
  0.0 0.7 %sign_compare_fusion = pred[3072]{0:T(1024)(128)(4,1)S(1)} fusion(s32[3072]{0:T(1024)} %param.9), kind=kLoop, calls=%fused_computation.6 | loop fusion | flops 6144 | bytes 15360 | tf_op jit(solution)/shard_map/jit(floor_divide)/ne | solution.py:321
  0.7 0.1 ne.27
  0.8 0.7 %broadcast_remainder_fusion = (s32[3072]{0:T(1024)S(1)}, s32[3072]{0:T(1024)S(1)}) fusion(s32[3072]{0:T(1024)} %param.9), kind=kLoop, calls=%fused_computation.8 | loop fusion | flops 6144 | bytes 36864 | tf_op jit(solution)/shard_map/jit(floor_divide)/rem | solution.py:321
  1.5 0.1 rem.19
  1.6 0.1 div.10
  1.7 0.7 %fusion.2 = s32[32,96]{1,0:T(8,128)S(1)} fusion(s32[32,96]{1,0:T(8,128)S(1)} %div.10, s32[32,96]{1,0:T(8,128)S(1)} %rem.19, pred[32,96]{1,0:T(8,128)(4,1)S(1)} %ne.27, s32[32]{0:T(128)} %param.10), kind=kLoop, calls=%fused_computation.4 | loop fusion | flops 36864 | bytes 40064 | tf_op jit(solution)/shard_map/jit(_where)/select_n | solution.py:321
  2.4 0.6 %pad.4 = s32[32,128]{1,0:T(8,128)} pad(s32[32,96]{1,0:T(8,128)S(1)} %fusion.2, s32[]{:T(128)} %constant.21.clone.1), padding=0_0x0_32 | pad | bytes 28676 | tf_op jit(solution)/shard_map/jit(_pad)/pad | solution.py:322
  3.0 51.4 %shard_map.82 = bf16[24,96,256]{2,1,0:T(8,128)(2,1)} custom-call(bf16[32,96,128]{2,1,0:T(8,128)(2,1)} %bitcast.7, s32[32,1,128]{2,1,0:T(1,128)} %bitcast.8, f32[3,3]{1,0:T(4,128)} %spread.1, bf16[128,256]{1,0:T(8,128)(2,1)} %w_in.1, f32[1,256]{1,0:T(1,128)} %bitcast.9, bf16[2304,256]{1,0:T(8,128)(2,1)} %bitcast.5, bf16[2304,256]{1,0:T(8,128)(2,1)} %bitcast.6), custom_call_target="tpu_custom_call" | custom-call | tf_op jit(solution)/shard_map/pallas_call | solution.py:327
  54.4 2.4 %copy.10 = bf16[24,96,256]{2,1,0:T(8,128)(2,1)} copy(bf16[24,96,256]{2,1,0:T(8,128)(2,1)} %shard_map.82) | data formatting | bytes 2359296

commit v2 on v1

--- a/solution.py
+++ b/solution.py
@@ -34,10 +34,10 @@
 
 def kernel(
     lat_n, lon_n,
-    feats, cells, spread, w_in, w_dens, w_one, w_two, out,
-    rows_in, cells_in, lhs, acc, mean, logd, grid_x, hid_x, win_v, wone_v, wtwo_v,
+    feats, raw, used, spread, w_in, w_dens, w_one, w_two, out,
+    cells, out_v, rows_in, cells_in, lhs, acc, mean, logd, grid_x, hid_x, win_v, wone_v, wtwo_v,
     row_out, row_in, col_out, col_in, corner_in,
-    row_send, row_recv, cell_send, cell_recv, own_sem, w_sem, halo_send, halo_recv,
+    row_send, row_recv, cell_send, cell_recv, own_sem, w_sem, out_sem, halo_send, halo_recv,
 ):
     n = lat_n * lon_n
     groups = n // GROUP
@@ -58,6 +58,22 @@
             barrier, inc=1, device_id=(peer // lon_n, peer % lon_n), device_id_type=MESH
         )
 
+    lane = lax.broadcasted_iota(jnp.int32, (1, 128), 1)
+
+    @pl.loop(0, n // 4)
+    def _(quad):
+        one, two, three = (raw[pl.ds(3 * quad + k, 1)] for k in range(3))
+        picks = [
+            one,
+            jnp.where(lane < 32, pltpu.roll(one, 32, 1), pltpu.roll(two, 32, 1)),
+            jnp.where(lane < 64, pltpu.roll(two, 64, 1), pltpu.roll(three, 64, 1)),
+            pltpu.roll(three, 96, 1),
+        ]
+        for k, pick in enumerate(picks):
+            row = ((pick.astype(F32) + 0.5) * (1.0 / PW)).astype(jnp.int32)
+            code = row * 128 + (pick - row * PW)
+            cells[4 * quad + k] = jnp.where(lane < used[4 * quad + k], code, 127 * 128)
+
     own = [
         pltpu.make_async_copy(feats.at[me], rows_in.at[me], own_sem.at[0]),
         pltpu.make_async_copy(cells.at[me], cells_in.at[me], own_sem.at[1]),
@@ -67,7 +83,7 @@
         pltpu.make_async_copy(w_one, wone_v, w_sem.at[1]),
         pltpu.make_async_copy(w_two, wtwo_v, w_sem.at[2]),
     ]
-    for item in own + weights:
+    for item in weights:
         item.start()
     pl.semaphore_wait(barrier, n - 1)
 
@@ -86,22 +102,24 @@
         )
 
     def peer_of(step):
-        turn = groups - 1 - step // GROUP
+        turn = 1 + step // GROUP
         return xor(my_group, turn, groups) * GROUP + (my_place + step % GROUP) % GROUP
 
     def each_peer(act):
+        for place in range(1, GROUP):
+            act(my_group * GROUP + (my_place + place) % GROUP)
+
         @pl.loop(0, n - GROUP)
         def _(step):
             act(peer_of(step))
 
-        for place in range(1, GROUP):
-            act(my_group * GROUP + (my_place + place) % GROUP)
-
     def send(peer):
         cell_copy(peer, me, peer).start()
         row_copy(peer, me, peer).start()
 
     each_peer(send)
+    for item in own:
+        item.start()
 
     acc[...] = jnp.zeros_like(acc)
 
@@ -126,14 +144,6 @@
             )
             acc[span] += part.reshape(HALF, PWP, C)
 
-    @pl.loop(0, groups - 1)
-    def _(step):
-        base = xor(my_group, groups - 1 - step, groups) * GROUP
-        for m in range(GROUP):
-            cell_copy(base + m, base + m, base + m).wait_recv()
-            row_copy(base + m, base + m, base + m).wait_recv()
-        add_group(base)
-
     for place in range(1, GROUP):
         peer = my_group * GROUP + (my_place + place) % GROUP
         cell_copy(peer, peer, peer).wait_recv()
@@ -141,6 +151,14 @@
     for item in own:
         item.wait()
     add_group(my_group * GROUP)
+
+    @pl.loop(1, groups)
+    def _(step):
+        base = xor(my_group, step, groups) * GROUP
+        for m in range(GROUP):
+            cell_copy(base + m, base + m, base + m).wait_recv()
+            row_copy(base + m, base + m, base + m).wait_recv()
+        add_group(base)
 
     weights[0].wait()
 
@@ -209,7 +227,7 @@
         last = x_ref[r, TW - 16 : TW, 2 * C :].astype(F32)
         x_ref[r, TW - 16 : TW, 2 * C :] = jnp.where(ids == 15, right, last).astype(BF16)
 
-    def exchange(stage, x_ref):
+    def exchange(stage, x_ref, beside):
         row_out[stage, 0] = x_ref[1, :, C : 2 * C]
         row_out[stage, 1] = x_ref[TH, :, C : 2 * C]
         both, to_up, to_down = copies(stage, x_ref)
@@ -226,10 +244,11 @@
             for item in to_down:
                 item.start()
 
+        beside()
         for item in both:
             item.wait_recv()
 
-        @pl.loop(0, TH)
+        @pl.loop(0, TH, unroll=4)
         def _(r):
             set_edges(
                 x_ref, r + 1, col_in[stage, 0, pl.ds(r, 1)], col_in[stage, 1, pl.ds(r, 1)]
@@ -284,7 +303,11 @@
         )
         return jnp.dot(window, weight[...], preferred_element_type=F32).reshape(ROWS, TW, C)
 
-    exchange(0, grid_x)
+    def sent(peer):
+        cell_copy(peer, me, peer).wait_send()
+        row_copy(peer, me, peer).wait_send()
+
+    exchange(0, grid_x, lambda: each_peer(sent))
     weights[1].wait()
 
     @pl.loop(0, TH // ROWS)
@@ -295,31 +318,30 @@
             value = total[k]
             put(hid_x, 1, start + k, value / (1.0 + jnp.exp(-value)))
 
-    exchange(1, hid_x)
+    exchange(1, hid_x, lambda: None)
     weights[2].wait()
+
+    def out_copy(start):
+        span = pl.ds(start, ROWS)
+        return pltpu.make_async_copy(out_v.at[span], out.at[span], out_sem.at[start // ROWS])
 
     @pl.loop(0, TH // ROWS)
     def _(step):
         start = step * ROWS
         total = conv(hid_x, wtwo_v, start)
         base = grid_x[pl.ds(start + 1, ROWS), :, C : 2 * C].astype(F32)
-        out[pl.ds(start, ROWS)] = (base + total).astype(BF16)
-
-    def sent(peer):
-        cell_copy(peer, me, peer).wait_send()
-        row_copy(peer, me, peer).wait_send()
-
-    each_peer(sent)
+        out_v[pl.ds(start, ROWS)] = (base + total).astype(BF16)
+        out_copy(start).start()
+
+    for step in range(TH // ROWS):
+        out_copy(step * ROWS).wait()
 
 
 def shards(features, cell_index, tile_rows, spread, w_in, w_dens, w_one, w_two):
     lat_n = lax.axis_size("lat")
     lon_n = lax.axis_size("lon")
     n = lat_n * lon_n
-    cell = cell_index.reshape(n, CAP)
-    used = jnp.arange(CAP, dtype=jnp.int32)[None, :] < tile_rows[:, None]
-    code = jnp.where(used, (cell // PW) * 128 + cell % PW, 127 * 128)
-    code = jnp.pad(code, ((0, 0), (0, 128 - CAP))).reshape(n, 1, 128)
+    hbm = pl.BlockSpec(memory_space=pltpu.HBM)
     anywhere = pl.BlockSpec(memory_space=pl.ANY)
     vmem = pl.BlockSpec(memory_space=pltpu.VMEM)
     smem = pl.BlockSpec(memory_space=pltpu.SMEM)
@@ -327,9 +349,11 @@
     return pl.pallas_call(
         functools.partial(kernel, lat_n, lon_n),
         out_shape=jax.ShapeDtypeStruct((TH, TW, C), BF16),
-        in_specs=[anywhere, anywhere, smem, anywhere, vmem, anywhere, anywhere],
-        out_specs=vmem,
+        in_specs=[hbm, vmem, smem, smem, hbm, vmem, hbm, hbm],
+        out_specs=anywhere,
         scratch_shapes=[
+            pltpu.VMEM((n, 1, 128), jnp.int32),
+            pltpu.VMEM((TH, TW, C), BF16),
             pltpu.VMEM((n, CAP, F), BF16),
             pltpu.VMEM((n, 1, 128), jnp.int32),
             pltpu.VMEM((PH, PWP, GROUP * CAP), BF16),
@@ -347,13 +371,13 @@
             pltpu.VMEM((2, 2, TH, C), F32),
             pltpu.VMEM((2, 4, 8, C), F32),
             dma((n,)), dma((n,)), dma((n,)), dma((n,)),
-            dma((2,)), dma((3,)), dma((2, 8)), dma((2, 8)),
+            dma((2,)), dma((3,)), dma((TH // ROWS,)), dma((2, 8)), dma((2, 8)),
         ],
         compiler_params=pltpu.CompilerParams(
             collective_id=0, has_side_effects=True, vmem_limit_bytes=60 * 1024 * 1024
         ),
     )(
-        features.reshape(n, CAP, F), code, spread, w_in, w_dens.reshape(1, C),
+        features.reshape(n, CAP, F), cell_index.reshape(-1, 128), tile_rows, spread, w_in, w_dens.reshape(1, C),
         w_one.reshape(9 * C, C), w_two.reshape(9 * C, C),
     )
 

time: 57.3 us -> 51.2 us (0.89)
  Pallas kernels: 51.4 us -> 48.6 us
  other arithmetic: 2.16 us -> 0 us
  local copies, waits for them, and re-layouts: 3.2 us -> 2.36 us
    pallas_call x1, Pallas kernels: 51.4 us -> 48.6 us  [shards(): pl.pallas_call(functools.partial(kernel, lat_n, lon_n), out_shape=jax.Sha...]
    select_n x1 -> x0, other arithmetic: 0.73 us -> none  [shards(): code = jnp.where(used, cell // PW * 128 + cell % PW, 127 * 128)]
    rem x1 -> x0, other arithmetic: 0.72 us -> none  [shards(): code = jnp.where(used, cell // PW * 128 + cell % PW, 127 * 128)]
    ne x1 -> x0, other arithmetic: 0.71 us -> none  [shards(): code = jnp.where(used, cell // PW * 128 + cell % PW, 127 * 128)]
    pad x1 -> x0, local copies, waits for them, and re-layouts: 0.61 us -> none  [shards(): code = jnp.pad(code, ((0, 0), (0, 128 - CAP))).reshape(n, 1, 128)]
where the time goes in v2:
time: 51.2 us; the launch traced here: 51 us
  Pallas kernels  48.6 us (95%)
  local copies, waits for them, and re-layouts  2.36 us (5%)
    pallas_call x1, Pallas kernels, shards(): pl.pallas_call(functools.partial(kernel, lat_n, lon_n), out_shape=jax.Sha...  48.6 us
    unnamed x1, local copies, waits for them, and re-layouts  2.36 us

profile of v2, /device:TPU:0, one launch (start us, length us, event | category | flops | bytes accessed | tf_op | source)
XLA Modules:
  0.0 51.0 jit_solution(7180642543793469124)
XLA Ops:
  0.0 48.6 %shard_map.82 = bf16[24,96,256]{2,1,0:T(8,128)(2,1)} custom-call(bf16[32,96,128]{2,1,0:T(8,128)(2,1)} %bitcast.7, s32[24,128]{1,0:T(8,128)} %bitcast.8, s32[32]{0:T(128)} %used.1, f32[3,3]{1,0:T(4,128)} %spread.1, bf16[128,256]{1,0:T(8,128)(2,1)} %w_in.1, f32[1,256]{1,0:T(1,128)} %bitcast.9, bf16[2304,256]{1,0:T(8,128)(2,1)} %bitcast.5, ...), custom_call_target="tpu_custom_call" | custom-call | tf_op jit(solution)/shard_map/pallas_call | solution.py:349
  48.6 2.4 %copy.10 = bf16[24,96,256]{2,1,0:T(8,128)(2,1)} copy(bf16[24,96,256]{2,1,0:T(8,128)(2,1)} %shard_map.82) | data formatting | bytes 2359296

commit v3 on v2

--- a/solution.py
+++ b/solution.py
@@ -17,7 +17,7 @@
 PWP = 112
 GROUP = 8
 HALF = PH // 2
-ROWS = 8
+ROWS = 12
 MESH = pl.DeviceIdType.MESH
 F32 = jnp.float32
 BF16 = jnp.bfloat16
@@ -169,7 +169,7 @@
         col_out[stage, 0, pl.ds(r, 1)] = value[0:1]
         col_out[stage, 1, pl.ds(r, 1)] = value[TW - 1 : TW]
 
-    @pl.loop(0, TH)
+    @pl.loop(0, TH, unroll=2)
     def _(r):
         parts = []
         for b in range(3):
@@ -248,10 +248,9 @@
         for item in both:
             item.wait_recv()
 
-        @pl.loop(0, TH, unroll=4)
-        def _(r):
+        for r in range(TH):
             set_edges(
-                x_ref, r + 1, col_in[stage, 0, pl.ds(r, 1)], col_in[stage, 1, pl.ds(r, 1)]
+                x_ref, r + 1, col_in[stage, 0, r : r + 1], col_in[stage, 1, r : r + 1]
             )
 
         def outer(r, side, corner_row):
@@ -284,6 +283,8 @@
         def _():
             x_ref[TH + 1] = jnp.zeros((TW, 3 * C), BF16)
 
+    def drain(stage, x_ref):
+        both, to_up, to_down = copies(stage, x_ref)
         for item in both:
             item.wait_send()
 
@@ -333,6 +334,8 @@
         out_v[pl.ds(start, ROWS)] = (base + total).astype(BF16)
         out_copy(start).start()
 
+    drain(0, grid_x)
+    drain(1, hid_x)
     for step in range(TH // ROWS):
         out_copy(step * ROWS).wait()
 

time: 51.2 us -> 50.6 us (0.988)
    pallas_call x1, Pallas kernels: 48.6 us -> 48.1 us  [shards(): pl.pallas_call(functools.partial(kernel, lat_n, lon_n), out_shape=jax.Sha...]
where the time goes in v3:
time: 50.6 us; the launch traced here: 50.4 us
  Pallas kernels  48.1 us (95%)
  local copies, waits for them, and re-layouts  2.36 us (5%)
    pallas_call x1, Pallas kernels, shards(): pl.pallas_call(functools.partial(kernel, lat_n, lon_n), out_shape=jax.Sha...  48.1 us
    unnamed x1, local copies, waits for them, and re-layouts  2.36 us

profile of v3, /device:TPU:0, one launch (start us, length us, event | category | flops | bytes accessed | tf_op | source)
XLA Modules:
  0.0 50.4 jit_solution(15707316369228924881)
XLA Ops:
  0.0 48.1 %shard_map.82 = bf16[24,96,256]{2,1,0:T(8,128)(2,1)} custom-call(bf16[32,96,128]{2,1,0:T(8,128)(2,1)} %bitcast.7, s32[24,128]{1,0:T(8,128)} %bitcast.8, s32[32]{0:T(128)} %used.1, f32[3,3]{1,0:T(4,128)} %spread.1, bf16[128,256]{1,0:T(8,128)(2,1)} %w_in.1, f32[1,256]{1,0:T(1,128)} %bitcast.9, bf16[2304,256]{1,0:T(8,128)(2,1)} %bitcast.5, ...), custom_call_target="tpu_custom_call" | custom-call | tf_op jit(solution)/shard_map/pallas_call | solution.py:352
  48.1 2.4 %copy.10 = bf16[24,96,256]{2,1,0:T(8,128)(2,1)} copy(bf16[24,96,256]{2,1,0:T(8,128)(2,1)} %shard_map.82) | data formatting | bytes 2359296
